TPU v7x, 512 devices: a whole 4x8x8 slice. The times are simulated.
512 devices in a mesh: owner: 32 (over y, x), rows: 16 (over z, core).
Axes of the slice: x: 4, y: 8, z: 8, core: 2. Of those that a mesh axis runs over, the one named last changes fastest.
Arguments:
- w_down: float32 [64, 1408, 2048], P('owner', None, 'rows'), may hold values from -0.21875 to 0.21875
- router_weight: float32 [2048, 64], P('rows', 'owner'), may hold values from -0.125 to 0.125
- router_gain: float32 [2048], P('rows'), may hold values from 0.25 to 1.75
Outputs:
- serve_down: bfloat16 [64, 1408, 2048], P('owner')
- scale_down: float32 [64, 1408], P('owner')
- serve_router: bfloat16 [2048, 64], replicated
All inputs are finite; a program needn't handle non-finite values. Where the computation divides by a largest or mean magnitude, that divisor is 1e-20 or more.
Results may differ from a plain program's by a relative error of at most 0.001.
Values may be sent and summed in bfloat16 or wider, within the bound.
A program may use at most 128 MiB of HBM per device.

v0:
```python
import jax
import jax.numpy as jnp
from jax import lax
from jax.sharding import PartitionSpec as P


def sent_to_all(x, axis):
    copies = jnp.broadcast_to(x, (lax.axis_size(axis), *x.shape))
    return lax.all_to_all(copies, axis, split_axis=0, concat_axis=0, tiled=True)


def of_everyone(x, axis):
    everything = sent_to_all(x, axis)
    return jnp.max(everything, axis=0)


def laid_out(pieces, dim):
    pieces = jnp.moveaxis(pieces, 0, dim)
    lengths = pieces.shape
    return pieces.reshape(*lengths[:dim], lengths[dim] * lengths[dim + 1], *lengths[dim + 2 :])


def collect(x, axis, dim):
    return laid_out(sent_to_all(x, axis), dim)


def on_device(w_down, router_weight, router_gain):
    scale_down = of_everyone(jnp.max(jnp.abs(w_down), axis=2), "rows")
    narrow_down = (w_down / jnp.expand_dims(scale_down, 2)).astype(jnp.bfloat16)
    serve_down = lax.all_gather(narrow_down, "rows", axis=2, tiled=True)
    part_router = (router_weight * router_gain[:, None]).astype(jnp.bfloat16)
    row_router = lax.all_gather(part_router, "rows", axis=0, tiled=True)
    serve_router = collect(row_router, "owner", 1)
    return (serve_down, scale_down, serve_router)


def solution(mesh):
    placed = (P("owner", None, "rows"), P("rows", "owner"), P("rows"))
    return jax.shard_map(
        on_device,
        mesh=mesh,
        in_specs=placed,
        out_specs=(P("owner", None, None), P("owner", None), P()),
        check_vma=False,
    )
```

profile of v0, /device:TPU:1, one launch (start us, length us, event | category | flops | bytes accessed | tf_op | source)
XLA Modules:
  0.0 126.5 jit_solution(15650277266331991324)
XLA Ops:
  7.2 0.0 copy-start
  7.2 0.0 all-gather.2.cloned.1.call-start
  7.2 1.9 %abs_reduce_fusion = f32[2,1408]{1,0:T(2,128)S(1)} fusion(f32[2,1408,128]{2,1,0:T(8,128)} %param.3), kind=kLoop, calls=%fused_computation.1 | loop fusion | flops 718080 | bytes 1453056 | tf_op jit(solution)/shard_map/reduce_max | solution.py:28
  9.2 21.2 %all_to_all.10 = f32[16,2,1408]{2,1,0:T(2,128)S(1)} all-to-all(f32[16,2,1408]{2,1,0:T(2,128)S(1)} %broadcast_in_dim.8), channel_id=1, replica_groups=mesh['owner'=32,'rows'=16] {'rows'}, dimensions={0} | all-to-all | bytes 360448 | tf_op jit(solution)/shard_map/all_to_all | solution.py:9
  30.4 0.1 reduce_max.19
  30.5 0.0 copy-done
  30.5 0.0 copy-start.1
  30.5 0.0 copy-start.2
  30.5 0.0 copy-start.3
  30.5 1.3 %divide_convert_fusion = bf16[2,1408,128]{2,1,0:T(8,128)(2,1)} fusion(f32[2,1408,128]{2,1,0:T(8,128)S(1)} %copy-done, f32[2,1408]{1,0:T(2,128)S(1)} %reduce_max.19), kind=kLoop, calls=%fused_computation | loop fusion | flops 720896 | bytes 2173952 | tf_op jit(solution)/shard_map/convert_element_type | solution.py:29
  31.8 0.0 all-gather.2.cloned.1.call-update
  31.9 0.0 copy-done.1
  31.9 0.0 copy-done.2
  31.9 0.0 copy-done.3
  31.9 14.6 %all_gather.7 = bf16[2048,2]{0,1:T(2,128)(2,1)S(1)} all-gather(bf16[128,2]{0,1:T(2,128)(2,1)S(1)} %multiply_convert_fusion), channel_id=1, replica_groups=mesh['owner'=32,'rows'=16] {'rows'}, dimensions={0}, use_global_device_ids=true | all-gather | bytes 8704 | tf_op jit(solution)/shard_map/all_gather | solution.py:32
  46.5 0.1 broadcast_in_dim.9
  46.7 21.1 %all_to_all.11 = bf16[32,2048,2]{1,2,0:T(2,128)(2,1)S(1)} all-to-all(bf16[32,2048,2]{1,2,0:T(2,128)(2,1)S(1)} %broadcast_in_dim.9), channel_id=1, replica_groups=mesh['owner'=32,'rows'=16] {'owner'}, dimensions={0} | all-to-all | bytes 524288 | tf_op jit(solution)/shard_map/all_to_all | solution.py:9
  67.8 0.8 reshape.11
  68.6 40.9 %all-gather.2.cloned.1.call-done = bf16[2,1408,2048]{2,1,0:T(8,128)(2,1)} async-done(((bf16[2,1408,128]{2,1,0:T(8,128)(2,1)}), bf16[2,1408,2048]{2,1,0:T(8,128)(2,1)}) %all-gather.2.cloned.1.call-update) | async-done | bytes 11534352 | tf_op jit(solution)/shard_map/all_gather | solution.py:30
  109.5 10.1 %copy.9 = bf16[2,1408,2048]{2,1,0:T(8,128)(2,1)} copy(bf16[2,1408,2048]{2,1,0:T(8,128)(2,1)} %all-gather.2.cloned.1.call-done) | data formatting | bytes 23068672
  (2 shorter events, 0.1 us)
Async XLA Ops:
  7.2 23.3 %copy-start = (f32[2,1408,128]{2,1,0:T(8,128)S(1)}, f32[2,1408,128]{2,1,0:T(8,128)}, u32[]{:S(2)}) copy-start(f32[2,1408,128]{2,1,0:T(8,128)} %param.3) | copy-start | bytes 4325380
  7.2 102.4 %all-gather.2.cloned.1.call-start = ((), (), s32[]{:S(2)}) async-start(), calls=%async_computation.2 | async-start | bytes 12255232 | tf_op jit(solution)/shard_map/all_gather | solution.py:30
  30.5 1.4 %copy-start.1 = (f32[2,1408]{1,0:T(2,128)}, f32[2,1408]{1,0:T(2,128)S(1)}, u32[]{:S(2)}) copy-start(f32[2,1408]{1,0:T(2,128)S(1)} %reduce_max.19) | copy-start | bytes 33796
  30.5 1.4 %copy-start.2 = (f32[128,2]{0,1:T(2,128)S(1)}, f32[128,2]{0,1:T(2,128)}, u32[]{:S(2)}) copy-start(f32[128,2]{0,1:T(2,128)} %param.4) | copy-start | bytes 3076
  30.5 1.4 %copy-start.3 = (f32[128]{0:T(128)S(1)}, f32[128]{0:T(128)}, u32[]{:S(2)}) copy-start(f32[128]{0:T(128)} %param.5) | copy-start | bytes 1540
Sparse Core Ops, SparseCore 0:
  32.0 77.4 all-gather.1
where the time goes:
time: 127 us; the launch traced here: 126 us
  blocking collectives  57 us (45%)
  waiting for transfers between devices  41 us (32%)
  between operations  14.1 us (11%)
  local copies, waits for them, and re-layouts  11.1 us (9%)
  other arithmetic  3.29 us (3%)
    all_to_all x2, blocking collectives, sent_to_all(): return lax.all_to_all(copies, axis, split_axis=0, concat_axis=0, tiled=True)  42.3 us
    all_gather x1, waiting for transfers between devices, on_device(): serve_down = lax.all_gather(narrow_down, 'rows', axis=2, tiled=True)  40.9 us
    all_gather x1, blocking collectives, on_device(): row_router = lax.all_gather(part_router, 'rows', axis=0, tiled=True)  14.6 us
    unnamed x9, local copies, waits for them, and re-layouts  10.1 us
  transfers between devices with their start and end apart: 1, of which 1 were waited for; matrix products, arithmetic and copies ran while one was open for 1% of the time, Pallas kernels for 0%

commit v1 on v0

--- a/solution.py
+++ b/solution.py
@@ -2,6 +2,13 @@
 import jax.numpy as jnp
 from jax import lax
 from jax.sharding import PartitionSpec as P
+
+
+def swapped_in(x, axis, d):
+    peers = lax.axis_size(axis)
+    blocks = jnp.stack([x for _ in range(peers)])
+    blocks = lax.all_to_all(blocks, axis, split_axis=0, concat_axis=0)
+    return jnp.concatenate(blocks, axis=d)
 
 
 def sent_to_all(x, axis):
@@ -27,7 +34,7 @@
 def on_device(w_down, router_weight, router_gain):
     scale_down = of_everyone(jnp.max(jnp.abs(w_down), axis=2), "rows")
     narrow_down = (w_down / jnp.expand_dims(scale_down, 2)).astype(jnp.bfloat16)
-    serve_down = lax.all_gather(narrow_down, "rows", axis=2, tiled=True)
+    serve_down = swapped_in(narrow_down, "rows", 2)
     part_router = (router_weight * router_gain[:, None]).astype(jnp.bfloat16)
     row_router = lax.all_gather(part_router, "rows", axis=0, tiled=True)
     serve_router = collect(row_router, "owner", 1)

time: 127 us -> 353 us (2.78)
  waiting for transfers between devices: 41 us -> 261 us
  blocking collectives: 57 us -> 18 us
  starting transfers between devices: 0.04 us -> 29.8 us
  local copies, waits for them, and re-layouts: 11.1 us -> 39.8 us
  between operations: 14.1 us -> 0.71 us
    all_to_all x0 -> x3, waiting for transfers between devices: none -> 261 us  [the longest x1 250 us: swapped_in(): blocks = lax.all_to_all(blocks, axis, split_axis=0, concat_axis=0)]
    all_to_all x2 -> x0, blocking collectives: 42.3 us -> none  [sent_to_all(): return lax.all_to_all(copies, axis, split_axis=0, concat_axis=0, tiled=True)]
    all_gather x1 -> x0, waiting for transfers between devices: 40.9 us -> none  [on_device(): serve_down = lax.all_gather(narrow_down, 'rows', axis=2, tiled=True)]
    all_to_all x0 -> x3, starting transfers between devices: none -> 29.8 us  [the longest x2 21.5 us: sent_to_all(): return lax.all_to_all(copies, axis, split_axis=0, concat_axis=0, tiled=True)]
    all_to_all x0 -> x1, local copies, waits for them, and re-layouts: none -> 15.2 us  [swapped_in(): blocks = lax.all_to_all(blocks, axis, split_axis=0, concat_axis=0)]
    another operation x0 -> x1, local copies, waits for them, and re-layouts: none -> 7.03 us  [swapped_in(): blocks = jnp.stack([x for _ in range(peers)])]
    unnamed x9, local copies, waits for them, and re-layouts: 10.1 us -> 15.3 us
  transfers between devices with their start and end apart: 1 -> 3, of which waited for: 1 -> 2; matrix products, arithmetic and copies ran while one was open for 1% -> 0% of each run, Pallas kernels for 0% -> 0%
where the time goes in v1:
time: 353 us; the launch traced here: 352 us
  waiting for transfers between devices  261 us (74%)
  local copies, waits for them, and re-layouts  39.8 us (11%)
  starting transfers between devices  29.8 us (8%)
  blocking collectives  18 us (5%)
    all_to_all x1, waiting for transfers between devices, swapped_in(): blocks = lax.all_to_all(blocks, axis, split_axis=0, concat_axis=0)  250 us
    all_to_all x2, starting transfers between devices, sent_to_all(): return lax.all_to_all(copies, axis, split_axis=0, concat_axis=0, tiled=True)  21.5 us
    all_gather x1, blocking collectives, on_device(): row_router = lax.all_gather(part_router, 'rows', axis=0, tiled=True)  18 us
    unnamed x9, local copies, waits for them, and re-layouts  15.3 us
    all_to_all x1, local copies, waits for them, and re-layouts, swapped_in(): blocks = lax.all_to_all(blocks, axis, split_axis=0, concat_axis=0)  15.2 us
    all_to_all x2, waiting for transfers between devices, sent_to_all(): return lax.all_to_all(copies, axis, split_axis=0, concat_axis=0, tiled=True)  11.1 us
    all_to_all x1, starting transfers between devices, swapped_in(): blocks = lax.all_to_all(blocks, axis, split_axis=0, concat_axis=0)  8.33 us
  transfers between devices with their start and end apart: 3, of which 2 were waited for; matrix products, arithmetic and copies ran while one was open for 0% of the time, Pallas kernels for 0%

profile of v1, /device:TPU:1, one launch (start us, length us, event | category | flops | bytes accessed | tf_op | source)
XLA Modules:
  0.0 351.9 jit_solution(5558363321905403555)
XLA Ops:
  0.6 0.0 copy-start
  0.6 0.0 copy-start.2
  0.7 0.0 copy-start.3
  0.7 1.9 abs_reduce_fusion
  2.6 0.7 broadcast_in_dim.8
  3.3 11.8 %all-to-all-start = ((f32[16,2,1408]{2,1,0:T(2,128)}), f32[16,2,1408]{2,1,0:T(2,128)S(1)}, u32[]{:S(2)}, u32[]{:S(2)}) async-start(f32[16,2,1408]{2,1,0:T(2,128)} %broadcast_in_dim.8), calls=%async_computation | async-start | bytes 360448 | tf_op jit(solution)/shard_map/all_to_all | solution.py:16
  15.1 0.0 copy-done.2
  15.1 0.0 copy-done.3
  15.2 18.0 %all_gather.3 = bf16[2048,2]{0,1:T(2,128)(2,1)S(1)} all-gather(bf16[128,2]{0,1:T(2,128)(2,1)S(1)} %multiply_convert_fusion), channel_id=1, replica_groups=mesh['owner'=32,'rows'=16] {'rows'}, dimensions={0}, use_global_device_ids=true | all-gather | bytes 8704 | tf_op jit(solution)/shard_map/all_gather | solution.py:39
  33.2 0.0 all-to-all-done
  33.2 0.8 broadcast_in_dim.9
  34.0 9.7 %all-to-all-start.2 = ((bf16[32,2048,2]{1,2,0:T(2,128)(2,1)}), bf16[32,2048,2]{1,2,0:T(2,128)(2,1)S(1)}, u32[]{:S(2)}, u32[]{:S(2)}) async-start(bf16[32,2048,2]{1,2,0:T(2,128)(2,1)} %broadcast_in_dim.9), calls=%async_computation.2 | async-start | bytes 524288 | tf_op jit(solution)/shard_map/all_to_all | solution.py:16
  43.7 0.1 reduce_max.19
  43.8 0.0 copy-done
  43.8 0.0 copy-start.1
  43.8 0.4 divide_convert_fusion
  44.2 11.1 %all-to-all-done.2 = bf16[32,2048,2]{1,2,0:T(2,128)(2,1)S(1)} async-done(((bf16[32,2048,2]{1,2,0:T(2,128)(2,1)}), bf16[32,2048,2]{1,2,0:T(2,128)(2,1)S(1)}, u32[]{:S(2)}, u32[]{:S(2)}) %all-to-all-start.2) | async-done | bytes 262176 | tf_op jit(solution)/shard_map/all_to_all | solution.py:16
  55.3 7.0 %stack.2 = bf16[16,2,1408,128]{3,2,1,0:T(8,128)(2,1)} broadcast(bf16[2,1408,128]{2,1,0:T(8,128)(2,1)S(1)} %divide_convert_fusion), dimensions={1,2,3} | broadcast | bytes 12255232 | tf_op jit(solution)/shard_map/stack | solution.py:9
  62.4 0.0 copy-done.1
  62.4 8.3 %all-to-all-start.1 = ((bf16[16,2,1408,128]{3,2,1,0:T(8,128)(2,1)}), bf16[16,2,1408,128]{3,2,1,0:T(8,128)(2,1)}, u32[]{:S(2)}, u32[]{:S(2)}) async-start(bf16[16,2,1408,128]{3,2,1,0:T(8,128)(2,1)} %stack.2), calls=%async_computation.1 | async-start | bytes 23068672 | tf_op jit(solution)/shard_map/all_to_all | solution.py:10
  70.7 0.8 reshape.21
  71.5 250.0 %all-to-all-done.1 = bf16[16,2,1408,128]{3,2,1,0:T(8,128)(2,1)} async-done(((bf16[16,2,1408,128]{3,2,1,0:T(8,128)(2,1)}), bf16[16,2,1408,128]{3,2,1,0:T(8,128)(2,1)}, u32[]{:S(2)}, u32[]{:S(2)}) %all-to-all-start.1) | async-done | bytes 11534368 | tf_op jit(solution)/shard_map/all_to_all | solution.py:10
  321.5 15.2 %copy.11 = bf16[16,2,1408,128]{2,3,0,1:T(8,128)(2,1)} copy(bf16[16,2,1408,128]{3,2,1,0:T(8,128)(2,1)} %all-to-all-done.1) | data formatting | bytes 23068672 | tf_op jit(solution)/shard_map/all_to_all | solution.py:10
  336.7 15.2 %copy.12 = bf16[2,1408,2048]{2,1,0:T(8,128)(2,1)} copy(bf16[2,1408,2048]{1,2,0:T(8,128)(2,1)} %bitcast.6) | data formatting | bytes 23068672
  (1 shorter events, 0.0 us)
Async XLA Ops:
  0.6 43.1 %copy-start = (f32[2,1408,128]{2,1,0:T(8,128)S(1)}, f32[2,1408,128]{2,1,0:T(8,128)}, u32[]{:S(2)}) copy-start(f32[2,1408,128]{2,1,0:T(8,128)} %param.3) | copy-start | bytes 4325380
  0.6 14.5 %copy-start.2 = (f32[128,2]{0,1:T(2,128)S(1)}, f32[128,2]{0,1:T(2,128)}, u32[]{:S(2)}) copy-start(f32[128,2]{0,1:T(2,128)} %param.4) | copy-start | bytes 3076
  0.7 14.5 %copy-start.3 = (f32[128]{0:T(128)S(1)}, f32[128]{0:T(128)}, u32[]{:S(2)}) copy-start(f32[128]{0:T(128)} %param.5) | copy-start | bytes 1540
  3.3 29.9 %all-to-all-start = ((f32[16,2,1408]{2,1,0:T(2,128)}), f32[16,2,1408]{2,1,0:T(2,128)S(1)}, u32[]{:S(2)}, u32[]{:S(2)}) async-start(f32[16,2,1408]{2,1,0:T(2,128)} %broadcast_in_dim.8), calls=%async_computation | async-start | bytes 360448 | tf_op jit(solution)/shard_map/all_to_all | solution.py:16
  34.0 21.3 %all-to-all-start.2 = ((bf16[32,2048,2]{1,2,0:T(2,128)(2,1)}), bf16[32,2048,2]{1,2,0:T(2,128)(2,1)S(1)}, u32[]{:S(2)}, u32[]{:S(2)}) async-start(bf16[32,2048,2]{1,2,0:T(2,128)(2,1)} %broadcast_in_dim.9), calls=%async_computation.2 | async-start | bytes 524288 | tf_op jit(solution)/shard_map/all_to_all | solution.py:16
  43.8 18.6 %copy-start.1 = (f32[2,1408]{1,0:T(2,128)}, f32[2,1408]{1,0:T(2,128)S(1)}, u32[]{:S(2)}) copy-start(f32[2,1408]{1,0:T(2,128)S(1)} %reduce_max.19) | copy-start | bytes 33796
  62.4 259.1 %all-to-all-start.1 = ((bf16[16,2,1408,128]{3,2,1,0:T(8,128)(2,1)}), bf16[16,2,1408,128]{3,2,1,0:T(8,128)(2,1)}, u32[]{:S(2)}, u32[]{:S(2)}) async-start(bf16[16,2,1408,128]{3,2,1,0:T(8,128)(2,1)} %stack.2), calls=%async_computation.1 | async-start | bytes 23068672 | tf_op jit(solution)/shard_map/all_to_all | solution.py:10
